TPU v7x, 32 devices: a whole 2x2x4 slice. The times are simulated.
32 devices in a mesh: row: 8 (over y, x, core), col: 4 (over z).
Axes of the slice: x: 2, y: 2, z: 4, core: 2. Of those that a mesh axis runs over, the one named last changes fastest.
Arguments:
- vectors: bfloat16 [32, 1024, 512], P('col', 'row'), may hold values from -6 to 6
- right_factors: bfloat16 [32, 32, 1024, 128], P('row', 'col'), may hold values from -0.1875 to 0.1875
- left_factors: bfloat16 [32, 32, 1024, 128], P('row', 'col'), may hold values from -0.125 to 0.125
- tile_ranks: int32 [32, 32], P('row', 'col'), may hold values from 16 to 128
- owner_map: int32 [32], replicated, may hold values from 0 to 31, as said below
Outputs:
- applied: bfloat16 [32, 1024, 512], P('row', 'col')
Inputs may be any that keep to these rules, and one draw needn't show every extreme that they name: owner_map is a permutation of 0 to 31; the 4 stored tile rows held by index i of row (stored rows i * 4 to i * 4 + 3) belong to 4 different indices of row of applied, i + c mod 8 for the same 4 offsets c at every i.
All inputs are finite; a program needn't handle non-finite values.
Results may differ from a plain program's by a relative error of at most 0.0066.
Values may be sent and summed in bfloat16 or wider, within the bound.
A program may use at most 128 MiB of HBM per device.

v0:
```python
import jax
import jax.numpy as jnp
from jax import lax
from jax.sharding import PartitionSpec as P


def masked_coeffs(products, tile_ranks, rank_width):
    columns = jnp.arange(rank_width, dtype=jnp.int32)
    kept_mask = columns[None, None, :] < tile_ranks[:, :, None]
    return jnp.where(kept_mask[:, :, :, None], products, 0.0).astype(jnp.bfloat16)


def build_buffer(payload, owner_map, cycle_size):
    held_rows = payload.shape[0]
    own_rows = lax.dynamic_slice_in_dim(owner_map, lax.axis_index("row") * held_rows, held_rows)
    target = own_rows // held_rows
    devices = jnp.arange(cycle_size, dtype=jnp.int32)
    matches = target[None, :] == devices[:, None]
    present = jnp.any(matches, axis=1)
    source_slot = jnp.sum(
        jnp.where(matches, jnp.arange(held_rows, dtype=jnp.int32)[None, :], 0), axis=1
    )
    picked = jnp.take(payload, source_slot, axis=0)
    return jnp.where(present[:, None, None], picked, jnp.zeros_like(picked))


def pick_rows(received, owner_map, held_rows):
    wanted = lax.axis_index("row") * held_rows + jnp.arange(held_rows, dtype=jnp.int32)
    matches = owner_map[None, :] == wanted[:, None]
    anchor = jnp.sum(
        jnp.where(matches, jnp.arange(owner_map.shape[0], dtype=jnp.int32)[None, :], 0), axis=1
    )
    return jnp.take(received, anchor // held_rows, axis=0)


def on_device(vectors, right_factors, left_factors, tile_ranks, owner_map):
    held_rows = right_factors.shape[0]
    rank_width = right_factors.shape[3]
    cycle_size = lax.axis_size("row")
    products = jnp.einsum(
        "ikbr,kbv->ikrv",
        right_factors,
        lax.all_gather(vectors, "row", axis=1, tiled=True),
        preferred_element_type=jnp.float32,
    )
    coeffs = masked_coeffs(products, tile_ranks, rank_width)
    partial_rows = jnp.einsum(
        "ikbr,ikrv->ibv", left_factors, coeffs, preferred_element_type=jnp.float32
    )
    summed = lax.psum_scatter(partial_rows, "col", scatter_dimension=1, tiled=True).astype(
        jnp.bfloat16
    )
    buffer = build_buffer(summed, owner_map, cycle_size)
    received = lax.all_to_all(buffer, "row", split_axis=0, concat_axis=0, tiled=True)
    applied = pick_rows(received, owner_map, held_rows)
    return applied


def solution(mesh):
    placed = (
        P("col", "row", None),
        P("row", "col", None, None),
        P("row", "col", None, None),
        P("row", "col"),
        P(),
    )
    return jax.shard_map(
        on_device, mesh=mesh, in_specs=placed, out_specs=P("row", "col", None), check_vma=False
    )
```

profile of v0, /device:TPU:0, one launch (start us, length us, event | category | flops | bytes accessed | tf_op | source)
XLA Modules:
  0.0 271.4 jit_solution(948302696471374495)
XLA Ops:
  6.5 0.0 all-gather.2.cloned.1.call-start
  6.5 0.7 all-gather.2.cloned.1.call-update
  7.3 0.0 reduce-scatter.2.cloned.1.call-start
  7.3 0.8 iota_compare_fusion
  8.1 58.2 %all-gather.2.cloned.1.call-done = bf16[8,1024,512]{2,1,0:T(8,128)(2,1)} async-done(((bf16[8,128,512]{2,1,0:T(8,128)(2,1)}), bf16[8,1024,512]{2,1,0:T(8,128)(2,1)}) %all-gather.2.cloned.1.call-update) | async-done | bytes 8388624 | tf_op jit(solution)/shard_map/all_gather | solution.py:43
  66.3 17.0 %fusion.7 = f32[4,1024,512]{1,2,0:T(8,128)} fusion(bf16[4,8,1024,128]{3,2,1,0:T(8,128)(2,1)} %param.7, pred[4,8,128]{2,1,0:T(8,128)(4,1)S(1)} %iota_compare_fusion, bf16[4,8,1024,128]{3,2,1,0:T(8,128)(2,1)} %param.6, bf16[8,1024,512]{2,1,0:T(8,128)(2,1)} %all-gather.2.cloned.1.call-done), kind=kOutput, calls=%fused_computation.9 | convolution fusion | flops 8594128896 | bytes 33558528 | tf_op jit(solution)/shard_map/ikbr,ikrv->ibv/dot_general | solution.py:47
  83.3 0.0 copy-start
  83.3 0.0 reduce-scatter.2.cloned.1.call-update
  83.3 0.6 copy-done
  83.9 0.1 and_select_fusion.1
  84.0 0.1 select_reduce_fusion
  84.1 0.1 fusion.14
  84.2 143.9 %reduce-scatter.2.cloned.1.call-done = f32[4,256,512]{1,2,0:T(8,128)} async-done(((f32[4,1024,512]{1,2,0:T(8,128)}), f32[4,256,512]{1,2,0:T(8,128)}) %reduce-scatter.2.cloned.1.call-update) | async-done | bytes 2097168 | tf_op jit(solution)/shard_map/reduce_scatter | solution.py:50
  228.1 1.7 convert_element_type.7
  229.8 0.7 gather_fusion
  230.5 1.6 select_select_fusion
  232.1 3.7 %all-to-all-start = ((bf16[8,256,512]{1,2,0:T(8,128)(2,1)}), bf16[8,256,512]{1,2,0:T(8,128)(2,1)S(1)}, u32[]{:S(2)}, u32[]{:S(2)}) async-start(bf16[8,256,512]{1,2,0:T(8,128)(2,1)} %select_select_fusion), calls=%async_computation.1 | async-start | bytes 4194304 | tf_op jit(solution)/shard_map/all_to_all | solution.py:54
  235.8 0.2 select_reduce_fusion.1
  236.0 26.4 %all-to-all-done = bf16[8,256,512]{1,2,0:T(8,128)(2,1)S(1)} async-done(((bf16[8,256,512]{1,2,0:T(8,128)(2,1)}), bf16[8,256,512]{1,2,0:T(8,128)(2,1)S(1)}, u32[]{:S(2)}, u32[]{:S(2)}) %all-to-all-start) | async-done | bytes 2097184 | tf_op jit(solution)/shard_map/all_to_all | solution.py:54
  262.4 0.6 gather_fusion.1
  263.0 0.2 broadcast_select_fusion
  263.2 1.3 copy.7
  (7 shorter events, 0.1 us)
Async XLA Ops:
  6.5 59.7 %all-gather.2.cloned.1.call-start = ((), (), s32[]{:S(2)}) async-start(), calls=%async_computation.2 | async-start | bytes 9437184 | tf_op jit(solution)/shard_map/all_gather | solution.py:43
  7.3 220.8 %reduce-scatter.2.cloned.1.call-start = ((), (), s32[]{:S(2)}) async-start(), calls=%async_computation.3 | async-start | bytes 10485760 | tf_op jit(solution)/shard_map/reduce_scatter | solution.py:50
  83.3 0.7 copy-start
  232.1 30.3 %all-to-all-start = ((bf16[8,256,512]{1,2,0:T(8,128)(2,1)}), bf16[8,256,512]{1,2,0:T(8,128)(2,1)S(1)}, u32[]{:S(2)}, u32[]{:S(2)}) async-start(bf16[8,256,512]{1,2,0:T(8,128)(2,1)} %select_select_fusion), calls=%async_computation.1 | async-start | bytes 4194304 | tf_op jit(solution)/shard_map/all_to_all | solution.py:54
Sparse Core Ops, SparseCore 0:
  9.2 56.9 all-gather.1
  83.4 144.6 reduce-scatter.1
where the time goes:
time: 272 us; the launch traced here: 271 us
  waiting for transfers between devices  229 us (84%)
  matrix products  17 us (6%)
  between operations  13.4 us (5%)
  other arithmetic  4.76 us (2%)
  starting transfers between devices  3.7 us (1%)
  local copies, waits for them, and re-layouts  3.24 us (1%)
    reduce_scatter x1, waiting for transfers between devices, on_device(): lax.psum_scatter(partial_rows, 'col', scatter_dimension=1, tiled=True)  144 us
    all_gather x1, waiting for transfers between devices, on_device(): lax.all_gather(vectors, 'row', axis=1, tiled=True)  58.2 us
    all_to_all x1, waiting for transfers between devices, on_device(): lax.all_to_all(buffer, 'row', split_axis=0, concat_axis=0, tiled=True)  26.4 us
    dot_general x1, matrix products, on_device(): jnp.einsum('ikbr,ikrv->ibv', left_factors, coeffs, preferred_element_type...  17 us
  transfers between devices with their start and end apart: 3, of which 3 were waited for; matrix products, arithmetic and copies ran while one was open for 0% of the time, Pallas kernels for 0%

commit v1 on v0

v1 whole, which is shorter than its diff:
```python
import functools

import jax
import jax.numpy as jnp
from jax import lax
from jax.experimental import pallas as pl
from jax.experimental.pallas import tpu as pltpu
from jax.sharding import PartitionSpec as P

MESH = pl.DeviceIdType.MESH
LANES = 128
PIECES = 2


def kernel(n_row, n_col, n_chunk, owner_map, tile_ranks, vectors, right, left, out, *scratch):
    (gathered, right_raw, right_t, left_v, coeffs, own_part, z_send, z_recv, final, a_send) = scratch[:10]
    a_recv = scratch[10 : 10 + n_chunk]
    (load_sem, fac_sem, ag_ssem, ag_rsem, fw_ssem, fw_rsem, z_ssem, z_rsem, a_ssem, a_rsem) = scratch[
        10 + n_chunk :
    ]
    held, tiles, block, rank_width = right_raw.shape
    depth = vectors.shape[1]
    width = gathered.shape[3]
    quarter = out.shape[1]
    n_chip = n_row // 2
    per_piece = held // PIECES
    me = lax.axis_index("row")
    z = lax.axis_index("col")
    chip, core = me // 2, me % 2
    partner = me + 1 - 2 * core

    def own_load(v):
        return pltpu.make_async_copy(
            vectors.at[:, :, pl.ds(v * width, width)],
            gathered.at[v, :, pl.ds(pl.multiple_of(me * depth, depth), depth), :],
            load_sem.at[v],
        )

    for v in range(n_chunk):
        own_load(v).start()
    right_load = pltpu.make_async_copy(right, right_raw, fac_sem.at[0])
    left_load = pltpu.make_async_copy(left, left_v, fac_sem.at[1])
    right_load.start()
    left_load.start()

    barrier = pltpu.get_barrier_semaphore()
    for d in range(1, n_row):
        pl.semaphore_signal(barrier, inc=1, device_id=((me + d) % n_row, z), device_id_type=MESH)

    @pl.when(z > 0)
    def _():
        pl.semaphore_signal(barrier, inc=1, device_id=(me, z - 1), device_id_type=MESH)

    @pl.when(z < n_col - 1)
    def _():
        pl.semaphore_signal(barrier, inc=1, device_id=(me, z + 1), device_id_type=MESH)

    both = jnp.where(z > 0, 1, 0) + jnp.where(z < n_col - 1, 1, 0)
    pl.semaphore_wait(barrier, n_row - 1 + both)

    def rows_of(v, index):
        return gathered.at[v, :, pl.ds(pl.multiple_of(index * depth, depth), depth), :]

    def gather_copy(v, d, index):
        target = ((chip + d) % n_chip) * 2 + core
        return pltpu.make_async_remote_copy(
            src_ref=rows_of(v, index),
            dst_ref=rows_of(v, index),
            send_sem=ag_ssem.at[v, d - 1],
            recv_sem=ag_rsem.at[v, d - 1],
            device_id=(target, z),
            device_id_type=MESH,
        )

    def forward_copy(v, d, index):
        return pltpu.make_async_remote_copy(
            src_ref=rows_of(v, index),
            dst_ref=rows_of(v, index),
            send_sem=fw_ssem.at[v, d],
            recv_sem=fw_rsem.at[v, d],
            device_id=(partner, z),
            device_id_type=MESH,
        )

    def source(d, of_core):
        return ((chip + n_chip - d) % n_chip) * 2 + of_core

    def gather_start(v):
        own_load(v).wait()
        for d in range(1, n_chip):
            gather_copy(v, d, me).start()
        forward_copy(v, 0, me).start()

    def gather_forward(v):
        for d in range(1, n_chip):
            gather_copy(v, d, source(d, core)).wait_recv()
            forward_copy(v, d, source(d, core)).start()

    def gather_finish(v):
        for d in range(n_chip):
            forward_copy(v, d, source(d, 1 - core)).wait_recv()

    below, above = z, n_col - 1 - z
    skew = jnp.where(above > below, above - below, below - above)
    nearest = jnp.where(above > below, below, above)
    farthest = jnp.where(above > below, above, below)
    far_sign = jnp.where(above > below, 1, -1)

    def share_at(k):
        late = k - skew
        paired = z + (nearest - late // 2) * (1 - 2 * (late % 2))
        return jnp.where(k < skew, z + far_sign * (farthest - k), paired)

    def partial_rows(s, share):
        rows = pl.ds(pl.multiple_of(share * quarter, quarter), quarter)
        lhs = jnp.concatenate([left_v[s, j, rows, :] for j in range(tiles)], axis=1)
        return jnp.dot(
            lhs, coeffs[s].reshape(tiles * rank_width, width), preferred_element_type=jnp.float32
        )

    def z_copy(v, share, piece, upward, target):
        span = pl.ds(piece * per_piece, per_piece)
        return pltpu.make_async_remote_copy(
            src_ref=z_send.at[v, share, span],
            dst_ref=z_recv.at[upward, v, share, span],
            send_sem=z_ssem.at[v, share, piece],
            recv_sem=z_rsem.at[upward, v, share, piece],
            device_id=(me, target),
            device_id_type=MESH,
        )

    def project(v):
        def tile(j, _):
            products = jnp.dot(right_t[j], gathered[v, j], preferred_element_type=jnp.float32)
            ids = lax.broadcasted_iota(jnp.int32, (rank_width, width), 0)
            for s in range(held):
                part = products[s * rank_width : (s + 1) * rank_width]
                coeffs[s, j] = jnp.where(ids < tile_ranks[s, j], part, 0.0).astype(jnp.bfloat16)
            return 0

        lax.fori_loop(0, tiles, tile, 0)

    def send_shares(v):
        for k in range(n_col - 1):
            share = share_at(k)
            upward = jnp.where(share > z, 1, 0)
            target = z + 2 * upward - 1
            has_input = jnp.where(upward == 1, below, above) > 0
            for piece in range(PIECES):

                @pl.when(has_input)
                def _():
                    z_copy(v, share, piece, upward, target).wait_recv()

                    def row(s, _):
                        total = partial_rows(s, share) + z_recv[upward, v, share, s].astype(jnp.float32)
                        z_send[v, share, s] = total.astype(jnp.bfloat16)
                        return 0

                    lax.fori_loop(piece * per_piece, (piece + 1) * per_piece, row, 0)

                @pl.when(jnp.logical_not(has_input))
                def _():
                    def row(s, _):
                        z_send[v, share, s] = partial_rows(s, share).astype(jnp.bfloat16)
                        return 0

                    lax.fori_loop(piece * per_piece, (piece + 1) * per_piece, row, 0)

                z_copy(v, share, piece, upward, target).start()

    def own_share(v):
        def row(s, _):
            own_part[v, s] = partial_rows(s, z)
            return 0

        lax.fori_loop(0, held, row, 0)

    def exchange_copy(v, d):
        return pltpu.make_async_remote_copy(
            src_ref=a_send.at[v, d],
            dst_ref=a_recv[v].at[d],
            send_sem=a_ssem.at[v, d],
            recv_sem=a_rsem.at[v, d],
            device_id=((me + d) % n_row, z),
            device_id_type=MESH,
        )

    def finalize(v):
        for has_input, upward in ((below > 0, 1), (above > 0, 0)):

            @pl.when(has_input)
            def _():
                other = z + 1 - 2 * upward
                for piece in range(PIECES):
                    z_copy(v, z, piece, upward, other).wait_recv()

                def row(s, _):
                    own_part[v, s] = own_part[v, s] + z_recv[upward, v, z, s].astype(jnp.float32)
                    return 0

                lax.fori_loop(0, held, row, 0)

        for s in range(held):
            final[s] = own_part[v, s].astype(jnp.bfloat16)
        for d in range(n_row - 1, -1, -1):
            target = (me + d) % n_row
            slot = jnp.int32(0)
            for s in range(held):
                slot = jnp.where(owner_map[me * held + s] // held == target, s, slot)
            if d == 0:
                a_recv[v][0] = final[slot]
            else:
                a_send[v, d] = final[slot]
                exchange_copy(v, d).start()

    def write_rows(v):
        for d in range(1, n_row):
            exchange_copy(v, d).wait_recv()
        for k in range(held):
            wanted = me * held + k
            holder = jnp.int32(0)
            for s in range(n_row * held):
                holder = jnp.where(owner_map[s] == wanted, s // held, holder)
            shift = (me + n_row - holder) % n_row
            out[k, :, v * width : (v + 1) * width] = a_recv[v][shift]

    gather_start(0)
    if n_chunk > 1:
        gather_start(1)
    right_load.wait()

    def flip(j, _):
        for s in range(held):
            right_t[j, s * rank_width : (s + 1) * rank_width, :] = right_raw[s, j].T
        return 0

    lax.fori_loop(0, tiles, flip, 0)
    left_load.wait()
    gather_forward(0)
    for v in range(n_chunk):
        if v + 2 < n_chunk:
            gather_start(v + 2)
        gather_finish(v)
        project(v)
        send_shares(v)
        own_share(v)
        if v + 1 < n_chunk:
            gather_forward(v + 1)
        if v > 0:
            finalize(v - 1)
        if v > 1:
            write_rows(v - 2)
    finalize(n_chunk - 1)
    if n_chunk > 1:
        write_rows(n_chunk - 2)
    write_rows(n_chunk - 1)

    for v in range(n_chunk):
        for d in range(1, n_chip):
            gather_copy(v, d, me).wait_send()
        for d in range(n_chip):
            forward_copy(v, d, me).wait_send()
        for k in range(n_col - 1):
            for piece in range(PIECES):
                z_copy(v, share_at(k), piece, 0, z).wait_send()
        for d in range(1, n_row):
            exchange_copy(v, d).wait_send()


def on_device(n_row, n_col, vectors, right_factors, left_factors, tile_ranks, owner_map):
    held, tiles, block, rank_width = right_factors.shape
    width = LANES
    n_vec = vectors.shape[2]
    n_chunk = n_vec // width
    quarter = block // n_col
    n_chip = n_row // 2
    bf16, f32 = jnp.bfloat16, jnp.float32
    dma = pltpu.SemaphoreType.DMA
    smem = pl.BlockSpec(memory_space=pltpu.SMEM)
    hbm = pl.BlockSpec(memory_space=pl.ANY)
    return pl.pallas_call(
        functools.partial(kernel, n_row, n_col, n_chunk),
        out_shape=jax.ShapeDtypeStruct((held, quarter, n_vec), bf16),
        in_specs=[smem, smem, hbm, hbm, hbm],
        out_specs=pl.BlockSpec(memory_space=pltpu.VMEM),
        scratch_shapes=[
            pltpu.VMEM((n_chunk, tiles, block, width), bf16),
            pltpu.VMEM((held, tiles, block, rank_width), bf16),
            pltpu.VMEM((tiles, held * rank_width, block), bf16),
            pltpu.VMEM((held, tiles, block, rank_width), bf16),
            pltpu.VMEM((held, tiles, rank_width, width), bf16),
            pltpu.VMEM((n_chunk, held, quarter, width), f32),
            pltpu.VMEM((n_chunk, n_col, held, quarter, width), bf16),
            pltpu.VMEM((2, n_chunk, n_col, held, quarter, width), bf16),
            pltpu.VMEM((held, quarter, width), bf16),
            pltpu.VMEM((n_chunk, n_row, quarter, width), bf16),
        ]
        + [pltpu.VMEM((n_row, quarter, width), bf16) for _ in range(n_chunk)]
        + [
            dma((n_chunk,)),
            dma((2,)),
            dma((n_chunk, n_chip - 1)),
            dma((n_chunk, n_chip - 1)),
            dma((n_chunk, n_chip)),
            dma((n_chunk, n_chip)),
            dma((n_chunk, n_col, PIECES)),
            dma((2, n_chunk, n_col, PIECES)),
            dma((n_chunk, n_row)),
            dma((n_chunk, n_row)),
        ],
        compiler_params=pltpu.CompilerParams(
            collective_id=0, has_side_effects=True, vmem_limit_bytes=60 * 1024 * 1024
        ),
    )(owner_map, tile_ranks, vectors, right_factors, left_factors)


def solution(mesh):
    placed = (
        P("col", "row", None),
        P("row", "col", None, None),
        P("row", "col", None, None),
        P("row", "col"),
        P(),
    )
    body = functools.partial(on_device, mesh.shape["row"], mesh.shape["col"])
    return jax.shard_map(
        body, mesh=mesh, in_specs=placed, out_specs=P("row", "col", None), check_vma=False
    )
```

time: 272 us -> 110 us (0.40)
  waiting for transfers between devices: 229 us -> 0 us
  Pallas kernels: 0 us -> 108 us
  matrix products: 17 us -> 0 us
  between operations: 13.4 us -> 0.01 us
  other arithmetic: 4.76 us -> 0 us
  starting transfers between devices: 3.7 us -> 0 us
    reduce_scatter x1 -> x0, waiting for transfers between devices: 144 us -> none  [on_device(): lax.psum_scatter(partial_rows, 'col', scatter_dimension=1, tiled=True)]
    pallas_call x0 -> x1, Pallas kernels: none -> 108 us  [on_device(): pl.pallas_call(functools.partial(kernel, n_row, n_col, n_chunk), out_shap...]
    all_gather x1 -> x0, waiting for transfers between devices: 58.2 us -> none  [on_device(): lax.all_gather(vectors, 'row', axis=1, tiled=True)]
    all_to_all x1 -> x0, waiting for transfers between devices: 26.4 us -> none  [on_device(): lax.all_to_all(buffer, 'row', split_axis=0, concat_axis=0, tiled=True)]
    dot_general x1 -> x0, matrix products: 17 us -> none  [on_device(): jnp.einsum('ikbr,ikrv->ibv', left_factors, coeffs, preferred_element_type...]
    all_to_all x1 -> x0, starting transfers between devices: 3.66 us -> none  [on_device(): lax.all_to_all(buffer, 'row', split_axis=0, concat_axis=0, tiled=True)]
  transfers between devices with their start and end apart: 3 -> 0, of which waited for: 3 -> 0; matrix products, arithmetic and copies ran while one was open for 0% -> 0% of each run, Pallas kernels for 0% -> 0%
where the time goes in v1:
time: 110 us
  Pallas kernels  108 us (98%)
  local copies, waits for them, and re-layouts  2.26 us (2%)
    pallas_call x1, Pallas kernels, on_device(): pl.pallas_call(functools.partial(kernel, n_row, n_col, n_chunk), out_shap...  108 us
    unnamed x1, local copies, waits for them, and re-layouts  2.26 us

profile of v1, /device:TPU:0, one launch (start us, length us, event | category | flops | bytes accessed | tf_op | source)
XLA Modules:
  0.0 110.2 jit_solution(11656320278970183039)
XLA Ops:
  0.0 107.9 %shard_map.55 = bf16[4,256,512]{2,1,0:T(8,128)(2,1)} custom-call(s32[32]{0:T(128)} %owner_map.1, s32[4,8]{1,0:T(4,128)} %tile_ranks.1, bf16[8,128,512]{2,1,0:T(8,128)(2,1)} %vectors.1, bf16[4,8,1024,128]{3,2,1,0:T(8,128)(2,1)} %right.1, bf16[4,8,1024,128]{3,2,1,0:T(8,128)(2,1)} %left.1), custom_call_target="tpu_custom_call" | custom-call | tf_op jit(solution)/shard_map/pallas_call | solution.py:282
  107.9 2.3 %copy.7 = bf16[4,256,512]{2,1,0:T(8,128)(2,1)} copy(bf16[4,256,512]{2,1,0:T(8,128)(2,1)} %shard_map.55) | data formatting | bytes 2097152

commit v2 on v1

v2 whole, which is shorter than its diff:
```python
import functools

import jax
import jax.numpy as jnp
from jax import lax
from jax.experimental import pallas as pl
from jax.experimental.pallas import tpu as pltpu
from jax.sharding import PartitionSpec as P

MESH = pl.DeviceIdType.MESH
LANES = 128
PIECES = 2
PARTS = 4


def kernel(n_row, n_col, n_chunk, owner_map, tile_ranks, vectors, right, left, out, *scratch):
    (gathered, right_raw, right_t, left_v, coeffs, share_part, own_part, z_send, z_recv, final) = scratch[:10]
    a_send = scratch[10]
    a_recv = scratch[11 : 11 + n_chunk]
    (load_sem, fac_sem, ag_ssem, ag_rsem, fw_ssem, fw_rsem, z_ssem, z_rsem, a_ssem, a_rsem) = scratch[
        11 + n_chunk :
    ]
    held, tiles, block, rank_width = right_raw.shape
    depth = vectors.shape[1]
    width = gathered.shape[3]
    quarter = out.shape[1]
    n_chip = n_row // 2
    per_piece = quarter // PIECES
    first_tiles = tiles // PARTS
    last = n_chunk - 1
    me = lax.axis_index("row")
    z = lax.axis_index("col")
    chip, core = me // 2, me % 2
    partner = me + 1 - 2 * core

    def own_load(v):
        return pltpu.make_async_copy(
            vectors.at[:, :, pl.ds(v * width, width)],
            gathered.at[v, :, pl.ds(pl.multiple_of(me * depth, depth), depth), :],
            load_sem.at[v],
        )

    for v in range(n_chunk):
        own_load(v).start()
    right_load = pltpu.make_async_copy(right, right_raw, fac_sem.at[0])
    left_load = pltpu.make_async_copy(left, left_v, fac_sem.at[1])
    right_load.start()
    left_load.start()

    barrier = pltpu.get_barrier_semaphore()
    for d in range(1, n_row):
        pl.semaphore_signal(barrier, inc=1, device_id=((me + d) % n_row, z), device_id_type=MESH)

    @pl.when(z > 0)
    def _():
        pl.semaphore_signal(barrier, inc=1, device_id=(me, z - 1), device_id_type=MESH)

    @pl.when(z < n_col - 1)
    def _():
        pl.semaphore_signal(barrier, inc=1, device_id=(me, z + 1), device_id_type=MESH)

    both = jnp.where(z > 0, 1, 0) + jnp.where(z < n_col - 1, 1, 0)
    pl.semaphore_wait(barrier, n_row - 1 + both)

    def parts_of(v):
        return PARTS if v == 0 else 1

    def slot_of(v, h):
        return h if v == 0 else PARTS - 1 + v

    def rows_of(v, h, index):
        span = pl.ds(h * first_tiles, first_tiles) if v == 0 else pl.ds(0, tiles)
        return gathered.at[v, span, pl.ds(pl.multiple_of(index * depth, depth), depth), :]

    def gather_copy(v, h, d, index):
        target = ((chip + d) % n_chip) * 2 + core
        return pltpu.make_async_remote_copy(
            src_ref=rows_of(v, h, index),
            dst_ref=rows_of(v, h, index),
            send_sem=ag_ssem.at[slot_of(v, h), d - 1],
            recv_sem=ag_rsem.at[slot_of(v, h), d - 1],
            device_id=(target, z),
            device_id_type=MESH,
        )

    def forward_copy(v, h, d, index):
        return pltpu.make_async_remote_copy(
            src_ref=rows_of(v, h, index),
            dst_ref=rows_of(v, h, index),
            send_sem=fw_ssem.at[slot_of(v, h), d],
            recv_sem=fw_rsem.at[slot_of(v, h), d],
            device_id=(partner, z),
            device_id_type=MESH,
        )

    def source(d, of_core):
        return ((chip + n_chip - d) % n_chip) * 2 + of_core

    def gather_start(v):
        own_load(v).wait()
        for h in range(parts_of(v)):
            for d in range(1, n_chip):
                gather_copy(v, h, d, me).start()
            forward_copy(v, h, 0, me).start()

    def gather_forward(v, h):
        for d in range(1, n_chip):
            gather_copy(v, h, d, source(d, core)).wait_recv()
            forward_copy(v, h, d, source(d, core)).start()

    def gather_finish(v, h):
        for d in range(n_chip):
            forward_copy(v, h, d, source(d, 1 - core)).wait_recv()

    below, above = z, n_col - 1 - z
    skew = jnp.where(above > below, above - below, below - above)
    nearest = jnp.where(above > below, below, above)
    farthest = jnp.where(above > below, above, below)
    far_sign = jnp.where(above > below, 1, -1)

    def share_at(k):
        late = k - skew
        paired = z + (nearest - late // 2) * far_sign * (2 * (late % 2) - 1)
        return jnp.where(k < skew, z + far_sign * (farthest - k), paired)

    def partial_rows(s, share):
        rows = pl.ds(pl.multiple_of(share * quarter, quarter), quarter)
        lhs = jnp.concatenate([left_v[s, j, rows, :] for j in range(tiles)], axis=1)
        return jnp.dot(
            lhs, coeffs[s].reshape(tiles * rank_width, width), preferred_element_type=jnp.float32
        )

    def z_copy(v, share, piece, upward, target):
        span = pl.ds(piece * per_piece, per_piece)
        return pltpu.make_async_remote_copy(
            src_ref=z_send.at[v, share, :, span, :],
            dst_ref=z_recv.at[upward, v, share, :, span, :],
            send_sem=z_ssem.at[v, share, piece],
            recv_sem=z_rsem.at[upward, v, share, piece],
            device_id=(me, target),
            device_id_type=MESH,
        )

    def project(v, first, count):
        def tile(j, _):
            products = jnp.dot(right_t[j], gathered[v, j], preferred_element_type=jnp.float32)
            ids = lax.broadcasted_iota(jnp.int32, (rank_width, width), 0)
            for s in range(held):
                part = products[s * rank_width : (s + 1) * rank_width]
                coeffs[s, j] = jnp.where(ids < tile_ranks[s, j], part, 0.0).astype(jnp.bfloat16)
            return 0

        lax.fori_loop(first, first + count, tile, 0)

    def send_shares(v):
        for k in range(n_col - 1):
            share = share_at(k)
            upward = jnp.where(share > z, 1, 0)
            target = z + 2 * upward - 1
            has_input = jnp.where(upward == 1, below, above) > 0

            def row(s, _):
                share_part[s] = partial_rows(s, share)
                return 0

            lax.fori_loop(0, held, row, 0)
            for piece in range(PIECES):
                span = slice(piece * per_piece, (piece + 1) * per_piece)

                @pl.when(has_input)
                def _():
                    z_copy(v, share, piece, upward, target).wait_recv()
                    for s in range(held):
                        total = share_part[s, span] + z_recv[upward, v, share, s, span].astype(jnp.float32)
                        z_send[v, share, s, span] = total.astype(jnp.bfloat16)

                @pl.when(jnp.logical_not(has_input))
                def _():
                    for s in range(held):
                        z_send[v, share, s, span] = share_part[s, span].astype(jnp.bfloat16)

                z_copy(v, share, piece, upward, target).start()

    def own_share(v):
        def row(s, _):
            own_part[v, s] = partial_rows(s, z)
            return 0

        lax.fori_loop(0, held, row, 0)

    def cuts_of(v):
        return PIECES if v == last else 1

    def exchange_copy(v, cut, d):
        size = quarter // cuts_of(v)
        span = pl.ds(cut * size, size)
        return pltpu.make_async_remote_copy(
            src_ref=a_send.at[v, d, span, :],
            dst_ref=a_recv[v].at[d, span, :],
            send_sem=a_ssem.at[v + cut, d],
            recv_sem=a_rsem.at[v + cut, d],
            device_id=((me + d) % n_row, z),
            device_id_type=MESH,
        )

    def finalize(v):
        slots = []
        for d in range(n_row):
            target = (me + d) % n_row
            slot = jnp.int32(0)
            for s in range(held):
                slot = jnp.where(owner_map[me * held + s] // held == target, s, slot)
            slots.append(slot)
        size = quarter // cuts_of(v)
        for cut in range(cuts_of(v)):
            span = slice(cut * size, (cut + 1) * size)
            for has_input, upward in ((below > 0, 1), (above > 0, 0)):

                @pl.when(has_input)
                def _():
                    other = z + 1 - 2 * upward
                    for piece in range(PIECES):
                        if piece * per_piece // size == cut:
                            z_copy(v, z, piece, upward, other).wait_recv()
                    for s in range(held):
                        own_part[v, s, span] = own_part[v, s, span] + z_recv[upward, v, z, s, span].astype(
                            jnp.float32
                        )

            for s in range(held):
                final[s, span] = own_part[v, s, span].astype(jnp.bfloat16)
            for d in range(n_row - 1, -1, -1):
                if d == 0:
                    a_recv[v][0, span] = final[slots[d], span]
                else:
                    a_send[v, d, span] = final[slots[d], span]
                    exchange_copy(v, cut, d).start()

    def write_rows(v):
        for cut in range(cuts_of(v)):
            for d in range(1, n_row):
                exchange_copy(v, cut, d).wait_recv()
        for k in range(held):
            wanted = me * held + k
            holder = jnp.int32(0)
            for s in range(n_row * held):
                holder = jnp.where(owner_map[s] == wanted, s // held, holder)
            shift = (me + n_row - holder) % n_row
            out[k, :, v * width : (v + 1) * width] = a_recv[v][shift]

    gather_start(0)
    right_load.wait()

    def flip(j, _):
        for s in range(held):
            right_t[j, s * rank_width : (s + 1) * rank_width, :] = right_raw[s, j].T
        return 0

    lax.fori_loop(0, tiles, flip, 0)
    left_load.wait()
    for v in range(n_chunk):
        if v == 0:
            for h in range(PARTS):
                gather_forward(0, h)
                if h == PARTS - 1 and n_chunk > 1:
                    gather_start(1)
                gather_finish(0, h)
                project(0, h * first_tiles, first_tiles)
        else:
            gather_finish(v, 0)
            project(v, 0, tiles)
        send_shares(v)
        own_share(v)
        if v + 1 < n_chunk:
            gather_forward(v + 1, 0)
        if v + 2 < n_chunk:
            gather_start(v + 2)
        if v > 0:
            finalize(v - 1)
        if v > 1:
            write_rows(v - 2)
    if n_chunk > 1:
        finalize(last)
        write_rows(last - 1)
    else:
        finalize(last)
    write_rows(last)

    for v in range(n_chunk):
        for h in range(parts_of(v)):
            for d in range(1, n_chip):
                gather_copy(v, h, d, me).wait_send()
            for d in range(n_chip):
                forward_copy(v, h, d, me).wait_send()
        for k in range(n_col - 1):
            for piece in range(PIECES):
                z_copy(v, share_at(k), piece, 0, z).wait_send()
        for cut in range(cuts_of(v)):
            for d in range(1, n_row):
                exchange_copy(v, cut, d).wait_send()


def on_device(n_row, n_col, vectors, right_factors, left_factors, tile_ranks, owner_map):
    held, tiles, block, rank_width = right_factors.shape
    width = LANES
    n_vec = vectors.shape[2]
    n_chunk = n_vec // width
    quarter = block // n_col
    n_chip = n_row // 2
    bf16, f32 = jnp.bfloat16, jnp.float32
    dma = pltpu.SemaphoreType.DMA
    smem = pl.BlockSpec(memory_space=pltpu.SMEM)
    hbm = pl.BlockSpec(memory_space=pl.ANY)
    return pl.pallas_call(
        functools.partial(kernel, n_row, n_col, n_chunk),
        out_shape=jax.ShapeDtypeStruct((held, quarter, n_vec), bf16),
        in_specs=[smem, smem, hbm, hbm, hbm],
        out_specs=pl.BlockSpec(memory_space=pltpu.VMEM),
        scratch_shapes=[
            pltpu.VMEM((n_chunk, tiles, block, width), bf16),
            pltpu.VMEM((held, tiles, block, rank_width), bf16),
            pltpu.VMEM((tiles, held * rank_width, block), bf16),
            pltpu.VMEM((held, tiles, block, rank_width), bf16),
            pltpu.VMEM((held, tiles, rank_width, width), bf16),
            pltpu.VMEM((held, quarter, width), f32),
            pltpu.VMEM((n_chunk, held, quarter, width), f32),
            pltpu.VMEM((n_chunk, n_col, held, quarter, width), bf16),
            pltpu.VMEM((2, n_chunk, n_col, held, quarter, width), bf16),
            pltpu.VMEM((held, quarter, width), bf16),
            pltpu.VMEM((n_chunk, n_row, quarter, width), bf16),
        ]
        + [pltpu.VMEM((n_row, quarter, width), bf16) for _ in range(n_chunk)]
        + [
            dma((n_chunk,)),
            dma((2,)),
            dma((n_chunk + PARTS - 1, n_chip - 1)),
            dma((n_chunk + PARTS - 1, n_chip - 1)),
            dma((n_chunk + PARTS - 1, n_chip)),
            dma((n_chunk + PARTS - 1, n_chip)),
            dma((n_chunk, n_col, PIECES)),
            dma((2, n_chunk, n_col, PIECES)),
            dma((n_chunk + PIECES - 1, n_row)),
            dma((n_chunk + PIECES - 1, n_row)),
        ],
        compiler_params=pltpu.CompilerParams(
            collective_id=0, has_side_effects=True, vmem_limit_bytes=60 * 1024 * 1024
        ),
    )(owner_map, tile_ranks, vectors, right_factors, left_factors)


def solution(mesh):
    placed = (
        P("col", "row", None),
        P("row", "col", None, None),
        P("row", "col", None, None),
        P("row", "col"),
        P(),
    )
    body = functools.partial(on_device, mesh.shape["row"], mesh.shape["col"])
    return jax.shard_map(
        body, mesh=mesh, in_specs=placed, out_specs=P("row", "col", None), check_vma=False
    )
```

time: 110 us -> 106 us (0.964)
  the two profiles are of different devices: /device:TPU:0 before, /device:TPU:16 now
where the time goes in v2:
time: 106 us
  Pallas kernels  103 us (97%)
  local copies, waits for them, and re-layouts  2.26 us (2%)
    pallas_call x1, Pallas kernels, on_device(): pl.pallas_call(functools.partial(kernel, n_row, n_col, n_chunk), out_shap...  103 us
    unnamed x1, local copies, waits for them, and re-layouts  2.26 us

profile of v2, /device:TPU:16, one launch (start us, length us, event | category | flops | bytes accessed | tf_op | source)
XLA Modules:
  0.0 105.6 jit_solution(8572346057358654835)
XLA Ops:
  0.0 103.4 %shard_map.55 = bf16[4,256,512]{2,1,0:T(8,128)(2,1)} custom-call(s32[32]{0:T(128)} %owner_map.1, s32[4,8]{1,0:T(4,128)} %tile_ranks.1, bf16[8,128,512]{2,1,0:T(8,128)(2,1)} %vectors.1, bf16[4,8,1024,128]{3,2,1,0:T(8,128)(2,1)} %right.1, bf16[4,8,1024,128]{3,2,1,0:T(8,128)(2,1)} %left.1), custom_call_target="tpu_custom_call" | custom-call | tf_op jit(solution)/shard_map/pallas_call | solution.py:314
  103.4 2.3 %copy.7 = bf16[4,256,512]{2,1,0:T(8,128)(2,1)} copy(bf16[4,256,512]{2,1,0:T(8,128)(2,1)} %shard_map.55) | data formatting | bytes 2097152
